TPU v7x, 32 devices: a whole 2x2x4 slice. The times are simulated.
32 devices in a mesh: row: 4 (over x, core), col: 8 (over z, y).
Axes of the slice: x: 2, y: 2, z: 4, core: 2. Of those that a mesh axis runs over, the one named last changes fastest.
Arguments:
- source_terms: float32 [256, 512, 256], P('row', 'col'), may hold values from -6 to 6
- initial_values: float32 [256, 512, 256], P('row', 'col'), may hold values from -6 to 6
- absorption: float32 [256, 512, 256], P('row', 'col'), may hold values from 0.1 to 0.9
Outputs:
- improved: float32 [256, 512, 256], P('row', 'col')
- remaining: float32 [256, 512, 256], P('row', 'col')
All inputs are finite; a program needn't handle non-finite values.
Results may differ from a plain program's by a relative error of at most 0.000043.
Values sent between devices are 32-bit elements; how exact they have to be, the bound alone decides.
A program may use at most 128 MiB of HBM per device.

v0:
```python
import functools

import jax
import jax.numpy as jnp
from jax import lax
from jax.experimental import pallas as pl
from jax.experimental.pallas import tpu as pltpu
from jax.sharding import PartitionSpec as P

RATIO = 4
INNER = 9
DEEP = 2
WIDE = 4
TILE = 8
LANES = 128
MESH = pl.DeviceIdType.MESH
SIDES = ((-1, 0), (1, 0), (0, -1), (0, 1))
CORNERS = ((-1, -1), (-1, 1), (1, -1), (1, 1))
AROUND = SIDES + CORNERS


def span(step, length, depth):
    if step == 0:
        return 0, 0, length
    if step < 0:
        return 0, length, depth
    return length - depth, -depth, depth


def kernel(rows, cols, ny, nx, nl, f_hbm, u_hbm, m_hbm, out_hbm, rem_hbm, a, b, c, f, m, w, cl, cm, cw, v0, v1, v5,
           send, recv, local):
    me_r, me_c = lax.axis_index("row"), lax.axis_index("col")
    cy, cx = ny // RATIO, nx // RATIO
    wide_x, wide_cx = nx + TILE, cx + TILE

    def device(dy, dx):
        return (lax.rem(me_r + (dy + rows), rows), lax.rem(me_c + (dx + cols), cols))

    barrier = pltpu.get_barrier_semaphore()
    for dy, dx in AROUND:
        pl.semaphore_signal(barrier, inc=1, device_id=device(dy, dx), device_id_type=MESH)

    used = [0]

    def send_to(dy, dx, src, dst, depth, length_y, length_x, off_src, off_dst):
        width = length_x + TILE
        y_from, y_to, y_n = span(dy, length_y, depth)
        x_from, x_to, x_n = span(dx, length_x, depth)
        if x_to < 0:
            x_to += width
        k = used[0]
        used[0] += 1
        copy = pltpu.make_async_remote_copy(
            src_ref=src.at[pl.ds(off_src + y_from, y_n), pl.ds(x_from, x_n), :],
            dst_ref=dst.at[pl.ds(off_dst + y_to, y_n), pl.ds(x_to, x_n), :],
            send_sem=send.at[k],
            recv_sem=recv.at[k],
            device_id=device(dy, dx),
            device_id_type=MESH,
        )
        copy.start()
        return copy

    def fine_sends(src, dst, off_src, depth, around):
        out = []
        for dy, dx in around:
            deep = 1 if dy != 0 and dx != 0 else depth
            out.append(send_to(dy, dx, src, dst, deep, ny, nx, off_src, DEEP))
        return out

    def coarse_sends(ref):
        return [send_to(dy, dx, ref, ref, WIDE, cy, cx, WIDE, WIDE) for dy, dx in CORNERS + SIDES]

    def finish(copies):
        for copy in copies:
            copy.wait()

    def inside(ref):
        return ref.at[pl.ds(DEEP, ny), pl.ds(0, nx), :]

    loads = []
    for k, (src, dst) in enumerate(((m_hbm, m), (u_hbm, a), (f_hbm, f))):
        copy = pltpu.make_async_copy(src, inside(dst), local.at[k])
        copy.start()
        loads.append(copy)
    pl.semaphore_wait(barrier, len(AROUND))
    first = fine_sends(u_hbm, a, 0, DEEP, AROUND)
    first += fine_sends(m_hbm, m, 0, 1, SIDES)
    first += fine_sends(f_hbm, f, 0, 1, SIDES)

    halves = [pl.ds(h * LANES, LANES) for h in range(nl // LANES)]

    def cross(src, r, lane, width):
        mid = src[r, :, lane]
        left = pltpu.roll(mid, 1, 0)
        right = pltpu.roll(mid, wide_x - 1, 0)
        total = (left + right)[:width] + (src[r - 1, pl.ds(0, width), lane] + src[r + 1, pl.ds(0, width), lane])
        return mid[:width], total

    def sweep(src, dst, low, high, width):
        def body(r, carry):
            for lane in halves:
                mid, total = cross(src, r, lane, width)
                part = pl.ds(0, width)
                dst[r, part, lane] = 0.2 * mid + w[r, part, lane] * (total + f[r, part, lane])
            return carry

        lax.fori_loop(DEEP + low, DEEP + high, body, 0)

    def defect(src, r, lane):
        mid, total = cross(src, r, lane, nx)
        part = pl.ds(0, nx)
        return f[r, part, lane] + total - (4.0 + m[r, part, lane]) * mid

    at_block = lax.broadcasted_iota(jnp.int32, (cx, nx), 0)
    of_cell = lax.broadcasted_iota(jnp.int32, (cx, nx), 1) // RATIO
    pool = jnp.where(at_block == of_cell, 1.0 / RATIO, 0.0).astype(jnp.float32)
    of_row = lax.broadcasted_iota(jnp.int32, (nx, cx), 0) // RATIO
    at_row = lax.broadcasted_iota(jnp.int32, (nx, cx), 1)
    unpool = jnp.where(of_row == at_row, 1.0, 0.0).astype(jnp.float32)

    def dot(left, right):
        return jnp.dot(left, right, precision=lax.Precision.HIGHEST, preferred_element_type=jnp.float32)

    loads[0].wait()

    def masses(j, carry):
        for lane in halves:
            rows4 = [m[DEEP + j * RATIO + i, pl.ds(0, nx), lane] for i in range(RATIO)]
            cm[WIDE + j, pl.ds(0, cx), lane] = dot(pool, (rows4[0] + rows4[1]) + (rows4[2] + rows4[3]))
        return carry

    lax.fori_loop(0, cy, masses, 0)
    loads[1].wait()
    loads[2].wait()
    finish(first)
    mass_copies = coarse_sends(cm)

    def factor(r, carry):
        for lane in halves:
            w[r, :, lane] = 0.8 / (4.0 + m[r, :, lane])
        return carry

    lax.fori_loop(DEEP - 1, DEEP + ny + 1, factor, 0)

    sweep(a, b, -1, ny + 1, wide_x)
    sweep(b, c, 0, ny, nx)
    finish(fine_sends(c, c, DEEP, DEEP, AROUND))
    sweep(c, b, -1, ny + 1, wide_x)

    def coarse_loads(j, carry):
        for lane in halves:
            d = [defect(b, DEEP + j * RATIO + i, lane) for i in range(RATIO)]
            cl[WIDE + j, pl.ds(0, cx), lane] = dot(pool, (d[0] + d[1]) + (d[2] + d[3]))
        return carry

    lax.fori_loop(0, cy, coarse_loads, 0)
    load_copies = coarse_sends(cl)
    finish(mass_copies)

    def coarse_factor(r, carry):
        cw[r] = 0.8 / (4.0 + cm[r])
        return carry

    lax.fori_loop(0, cy + 2 * WIDE, coarse_factor, 0)
    finish(load_copies)

    def coarse_first(r, carry):
        v0[r] = cw[r] * cl[r]
        return carry

    lax.fori_loop(0, cy + 2 * WIDE, coarse_first, 0)

    def coarse_sweep(src, dst, edge, width):
        def body(r, carry):
            mid = src[r]
            total = pltpu.roll(mid, 1, 0) + pltpu.roll(mid, wide_cx - 1, 0) + (src[r - 1] + src[r + 1])
            new = 0.2 * mid + cw[r] * (total + cl[r])
            dst[r, pl.ds(0, width), :] = new[:width]
            return carry

        lax.fori_loop(edge, cy + 2 * WIDE - edge, body, 0, unroll=2)

    src = v0
    done, edge = 1, 0
    while done < INNER:
        edge += 1
        done += 1
        if edge == WIDE and done < INNER:
            coarse_sweep(src, v5, edge, cx)
            finish(coarse_sends(v5))
            src, edge = v5, 0
        else:
            dst = v1 if src is v0 else v0
            coarse_sweep(src, dst, edge, wide_cx)
            src = dst
    coarse = src

    def correct(j, carry):
        for lane in halves:
            add = dot(unpool, coarse[WIDE + j, pl.ds(0, cx), lane])
            for i in range(RATIO):
                r = DEEP + j * RATIO + i
                a[r, pl.ds(0, nx), lane] = b[r, pl.ds(0, nx), lane] + add
        return carry

    lax.fori_loop(0, cy, correct, 0)
    finish(fine_sends(a, a, DEEP, DEEP, AROUND))
    sweep(a, b, -1, ny + 1, wide_x)
    sweep(b, c, 0, ny, nx)
    finish(fine_sends(c, c, DEEP, DEEP, AROUND))
    sweep(c, b, -1, ny + 1, wide_x)
    outs = []
    copy = pltpu.make_async_copy(inside(b), out_hbm, local.at[3])
    copy.start()
    outs.append(copy)
    chunks = 4
    size = ny // chunks
    for k in range(chunks):
        def rest(r, carry):
            for lane in halves:
                a[r, pl.ds(0, nx), lane] = defect(b, r, lane)
            return carry

        lax.fori_loop(DEEP + k * size, DEEP + (k + 1) * size, rest, 0)
        copy = pltpu.make_async_copy(
            a.at[pl.ds(DEEP + k * size, size), pl.ds(0, nx), :], rem_hbm.at[pl.ds(k * size, size)], local.at[4 + k])
        copy.start()
        outs.append(copy)
    finish(outs)


def solution(mesh):
    rows, cols = mesh.shape["row"], mesh.shape["col"]

    def local(source_terms, initial_values, absorption):
        ny, nx, nl = source_terms.shape
        fine = pltpu.VMEM((ny + 2 * DEEP, nx + TILE, nl), jnp.float32)
        coarse = pltpu.VMEM((ny // RATIO + 2 * WIDE, nx // RATIO + TILE, nl), jnp.float32)
        anywhere = pl.BlockSpec(memory_space=pl.ANY)
        result = jax.ShapeDtypeStruct((ny, nx, nl), jnp.float32)
        return pl.pallas_call(
            functools.partial(kernel, rows, cols, ny, nx, nl),
            out_shape=(result, result),
            in_specs=[anywhere] * 3,
            out_specs=(anywhere, anywhere),
            scratch_shapes=[fine] * 6 + [coarse] * 6 + [
                pltpu.SemaphoreType.DMA((72,)),
                pltpu.SemaphoreType.DMA((72,)),
                pltpu.SemaphoreType.DMA((8,)),
            ],
            compiler_params=pltpu.CompilerParams(
                collective_id=0, has_side_effects=True, vmem_limit_bytes=48 * 1024 * 1024),
            name="two_grids",
        )(source_terms, initial_values, absorption)

    spec = P("row", "col", None)
    return jax.shard_map(local, mesh=mesh, in_specs=(spec,) * 3, out_specs=(spec,) * 2, check_vma=False)
```

profile of v0, /device:TPU:0, one launch (start us, length us, event | category | flops | bytes accessed | tf_op | source)
XLA Modules:
  0.0 87.5 jit_solution(4052164749916367573)
XLA Ops:
  0.6 81.2 %two_grids.1 = (f32[64,64,256]{2,1,0:T(8,128)S(1)}, f32[64,64,256]{2,1,0:T(8,128)}) custom-call(f32[64,64,256]{2,1,0:T(8,128)} %f_hbm.1, f32[64,64,256]{2,1,0:T(8,128)} %u_hbm.1, f32[64,64,256]{2,1,0:T(8,128)} %m_hbm.1), custom_call_target="tpu_custom_call" | custom-call | tf_op jit(solution)/shard_map/two_grids/pallas_call | solution.py:242
  81.8 0.0 copy-start
  81.8 2.1 %copy.7 = f32[64,64,256]{2,1,0:T(8,128)} copy(f32[64,64,256]{2,1,0:T(8,128)S(1)} %get-tuple-element.4) | data formatting | bytes 8388608
  84.0 1.6 %copy-done = f32[64,64,256]{2,1,0:T(8,128)S(1)} copy-done((f32[64,64,256]{2,1,0:T(8,128)S(1)}, f32[64,64,256]{2,1,0:T(8,128)}, u32[]{:S(2)}) %copy-start) | copy-done | bytes 4194328
  85.5 2.0 %copy.8 = f32[64,64,256]{2,1,0:T(8,128)} copy(f32[64,64,256]{2,1,0:T(8,128)S(1)} %copy-done) | data formatting | bytes 8388608
Async XLA Ops:
  81.8 3.7 %copy-start = (f32[64,64,256]{2,1,0:T(8,128)S(1)}, f32[64,64,256]{2,1,0:T(8,128)}, u32[]{:S(2)}) copy-start(f32[64,64,256]{2,1,0:T(8,128)} %get-tuple-element.5) | copy-start | bytes 12582916
where the time goes:
time: 87.7 us; the launch traced here: 87.5 us
  Pallas kernels  81.2 us (93%)
  local copies, waits for them, and re-layouts  5.71 us (7%)
    pallas_call x1, Pallas kernels, local(): pl.pallas_call(functools.partial(kernel, rows, cols, ny, nx, nl), out_sha...  81.2 us
    unnamed x4, local copies, waits for them, and re-layouts  5.71 us

commit v1 on v0

--- a/solution.py
+++ b/solution.py
@@ -12,6 +12,7 @@
 DEEP = 2
 WIDE = 4
 TILE = 8
+UNROLL = 2
 LANES = 128
 MESH = pl.DeviceIdType.MESH
 SIDES = ((-1, 0), (1, 0), (0, -1), (0, 1))
@@ -68,8 +69,24 @@
             out.append(send_to(dy, dx, src, dst, deep, ny, nx, off_src, DEEP))
         return out
 
+    def corner_row(dy, dx, ref, i):
+        n = WIDE - 1 - i
+        k = used[0]
+        used[0] += 1
+        copy = pltpu.make_async_remote_copy(
+            src_ref=ref.at[pl.ds(WIDE + (i if dy < 0 else cy - 1 - i), 1), pl.ds(0 if dx < 0 else cx - n, n), :],
+            dst_ref=ref.at[pl.ds(WIDE + cy + i if dy < 0 else WIDE - 1 - i, 1), pl.ds(cx if dx < 0 else wide_cx - n, n), :],
+            send_sem=send.at[k],
+            recv_sem=recv.at[k],
+            device_id=device(dy, dx),
+            device_id_type=MESH,
+        )
+        copy.start()
+        return copy
+
     def coarse_sends(ref):
-        return [send_to(dy, dx, ref, ref, WIDE, cy, cx, WIDE, WIDE) for dy, dx in CORNERS + SIDES]
+        out = [corner_row(dy, dx, ref, i) for i in range(WIDE - 1) for dy, dx in CORNERS]
+        return out + [send_to(dy, dx, ref, ref, WIDE, cy, cx, WIDE, WIDE) for dy, dx in SIDES[2:] + SIDES[:2]]
 
     def finish(copies):
         for copy in copies:
@@ -97,15 +114,66 @@
         total = (left + right)[:width] + (src[r - 1, pl.ds(0, width), lane] + src[r + 1, pl.ds(0, width), lane])
         return mid[:width], total
 
-    def sweep(src, dst, low, high, width):
+    def full_row(src, dst, r, width):
+        for lane in halves:
+            mid, total = cross(src, r, lane, width)
+            part = pl.ds(0, width)
+            dst[r, part, lane] = 0.2 * mid + w[r, part, lane] * (total + f[r, part, lane])
+
+    def full_rows(src, dst, low, high, width):
+        def body(r, carry):
+            full_row(src, dst, DEEP + r, width)
+            full_row(src, dst, DEEP + ny - 1 - r, width)
+            return carry
+
+        lax.fori_loop(low, high, body, 0)
+
+    def middle(src, dst, low):
+        part = pl.ds(TILE, nx - 2 * TILE)
+
         def body(r, carry):
             for lane in halves:
-                mid, total = cross(src, r, lane, width)
-                part = pl.ds(0, width)
-                dst[r, part, lane] = 0.2 * mid + w[r, part, lane] * (total + f[r, part, lane])
-            return carry
-
-        lax.fori_loop(DEEP + low, DEEP + high, body, 0)
+                line = src[r, pl.ds(0, nx), lane]
+                beside = (pltpu.roll(line, 1, 0) + pltpu.roll(line, nx - 1, 0))[TILE:nx - TILE]
+                total = beside + (src[r - 1, part, lane] + src[r + 1, part, lane])
+                dst[r, part, lane] = 0.2 * line[TILE:nx - TILE] + w[r, part, lane] * (total + f[r, part, lane])
+            return carry
+
+        lax.fori_loop(DEEP + low, DEEP + ny - low, body, 0, unroll=UNROLL)
+
+    def edges(src, dst, low, halo):
+        last = pl.ds(nx - TILE, 2 * TILE)
+        begin = pl.ds(0, TILE)
+
+        def body(r, carry):
+            for lane in halves:
+                line = jnp.concatenate([src[r, pl.ds(nx - 2 * TILE, 3 * TILE), lane], src[r, pl.ds(0, 2 * TILE), lane]], axis=0)
+                size = 5 * TILE
+                beside = (pltpu.roll(line, 1, 0) + pltpu.roll(line, size - 1, 0))
+                at_end = beside[TILE:3 * TILE] + (src[r - 1, last, lane] + src[r + 1, last, lane])
+                at_end = 0.2 * line[TILE:3 * TILE] + w[r, last, lane] * (at_end + f[r, last, lane])
+                if halo:
+                    dst[r, last, lane] = at_end
+                else:
+                    dst[r, pl.ds(nx - TILE, TILE), lane] = at_end[:TILE]
+                at_begin = beside[3 * TILE:4 * TILE] + (src[r - 1, begin, lane] + src[r + 1, begin, lane])
+                dst[r, begin, lane] = 0.2 * line[3 * TILE:4 * TILE] + w[r, begin, lane] * (at_begin + f[r, begin, lane])
+            return carry
+
+        lax.fori_loop(DEEP + low, DEEP + ny - low, body, 0, unroll=UNROLL)
+
+    def first_sweep(src, dst, between):
+        middle(src, dst, 1)
+        between()
+        full_rows(src, dst, -1, 1, wide_x)
+        edges(src, dst, 1, True)
+
+    def second_sweep(src, dst):
+        full_rows(src, dst, 0, DEEP, nx)
+        edges(src, dst, DEEP, False)
+        copies = fine_sends(dst, dst, DEEP, DEEP, SIDES[2:] + CORNERS + SIDES[:2])
+        middle(src, dst, DEEP)
+        return copies
 
     def defect(src, r, lane):
         mid, total = cross(src, r, lane, nx)
@@ -131,22 +199,28 @@
         return carry
 
     lax.fori_loop(0, cy, masses, 0)
+    def factor(low, high, part):
+        def body(r, carry):
+            w[r, part, :] = 0.8 / (4.0 + m[r, part, :])
+            return carry
+
+        lax.fori_loop(low, high, body, 0)
+
+    factor(DEEP, DEEP + ny, pl.ds(0, nx))
     loads[1].wait()
     loads[2].wait()
-    finish(first)
-    mass_copies = coarse_sends(cm)
-
-    def factor(r, carry):
-        for lane in halves:
-            w[r, :, lane] = 0.8 / (4.0 + m[r, :, lane])
-        return carry
-
-    lax.fori_loop(DEEP - 1, DEEP + ny + 1, factor, 0)
-
-    sweep(a, b, -1, ny + 1, wide_x)
-    sweep(b, c, 0, ny, nx)
-    finish(fine_sends(c, c, DEEP, DEEP, AROUND))
-    sweep(c, b, -1, ny + 1, wide_x)
+    mass_copies = []
+
+    def arrived():
+        finish(first)
+        mass_copies.extend(coarse_sends(cm))
+        factor(DEEP, DEEP + ny, pl.ds(nx, TILE))
+        factor(DEEP - 1, DEEP, pl.ds(0, wide_x))
+        factor(DEEP + ny, DEEP + ny + 1, pl.ds(0, wide_x))
+
+    first_sweep(a, b, arrived)
+    copies = second_sweep(b, c)
+    first_sweep(c, b, lambda: finish(copies))
 
     def coarse_loads(j, carry):
         for lane in halves:
@@ -205,11 +279,10 @@
         return carry
 
     lax.fori_loop(0, cy, correct, 0)
-    finish(fine_sends(a, a, DEEP, DEEP, AROUND))
-    sweep(a, b, -1, ny + 1, wide_x)
-    sweep(b, c, 0, ny, nx)
-    finish(fine_sends(c, c, DEEP, DEEP, AROUND))
-    sweep(c, b, -1, ny + 1, wide_x)
+    copies = fine_sends(a, a, DEEP, DEEP, SIDES[2:] + CORNERS + SIDES[:2])
+    first_sweep(a, b, lambda: finish(copies))
+    copies = second_sweep(b, c)
+    first_sweep(c, b, lambda: finish(copies))
     outs = []
     copy = pltpu.make_async_copy(inside(b), out_hbm, local.at[3])
     copy.start()
@@ -245,8 +318,8 @@
             in_specs=[anywhere] * 3,
             out_specs=(anywhere, anywhere),
             scratch_shapes=[fine] * 6 + [coarse] * 6 + [
-                pltpu.SemaphoreType.DMA((72,)),
-                pltpu.SemaphoreType.DMA((72,)),
+                pltpu.SemaphoreType.DMA((112,)),
+                pltpu.SemaphoreType.DMA((112,)),
                 pltpu.SemaphoreType.DMA((8,)),
             ],
             compiler_params=pltpu.CompilerParams(

time: 87.7 us -> 79.3 us (0.904)
  Pallas kernels: 81.2 us -> 72.8 us
    pallas_call x1, Pallas kernels: 81.2 us -> 72.8 us  [local(): pl.pallas_call(functools.partial(kernel, rows, cols, ny, nx, nl), out_sha...]
where the time goes in v1:
time: 79.3 us; the launch traced here: 79.1 us
  Pallas kernels  72.8 us (92%)
  local copies, waits for them, and re-layouts  5.71 us (7%)
    pallas_call x1, Pallas kernels, local(): pl.pallas_call(functools.partial(kernel, rows, cols, ny, nx, nl), out_sha...  72.8 us
    unnamed x4, local copies, waits for them, and re-layouts  5.71 us

profile of v1, /device:TPU:0, one launch (start us, length us, event | category | flops | bytes accessed | tf_op | source)
XLA Modules:
  0.0 79.1 jit_solution(18226727000734794356)
XLA Ops:
  0.6 72.8 %two_grids.1 = (f32[64,64,256]{2,1,0:T(8,128)S(1)}, f32[64,64,256]{2,1,0:T(8,128)}) custom-call(f32[64,64,256]{2,1,0:T(8,128)} %f_hbm.1, f32[64,64,256]{2,1,0:T(8,128)} %u_hbm.1, f32[64,64,256]{2,1,0:T(8,128)} %m_hbm.1), custom_call_target="tpu_custom_call" | custom-call | tf_op jit(solution)/shard_map/two_grids/pallas_call | solution.py:315
  73.4 0.0 copy-start
  73.4 2.1 %copy.7 = f32[64,64,256]{2,1,0:T(8,128)} copy(f32[64,64,256]{2,1,0:T(8,128)S(1)} %get-tuple-element.4) | data formatting | bytes 8388608
  75.5 1.6 %copy-done = f32[64,64,256]{2,1,0:T(8,128)S(1)} copy-done((f32[64,64,256]{2,1,0:T(8,128)S(1)}, f32[64,64,256]{2,1,0:T(8,128)}, u32[]{:S(2)}) %copy-start) | copy-done | bytes 4194328
  77.1 2.0 %copy.8 = f32[64,64,256]{2,1,0:T(8,128)} copy(f32[64,64,256]{2,1,0:T(8,128)S(1)} %copy-done) | data formatting | bytes 8388608
Async XLA Ops:
  73.4 3.7 %copy-start = (f32[64,64,256]{2,1,0:T(8,128)S(1)}, f32[64,64,256]{2,1,0:T(8,128)}, u32[]{:S(2)}) copy-start(f32[64,64,256]{2,1,0:T(8,128)} %get-tuple-element.5) | copy-start | bytes 12582916
